TPU v7x, 16 devices: a 4x2x1 block of a 4x4x8 slice. The times are simulated.
16 devices in a mesh: batch: 2 (over y, z), dap: 8 (over x, core).
Axes of the slice: x: 4, y: 2, z: 1, core: 2. Of those that a mesh axis runs over, the one named last changes fastest.
The devices are a block of a 4x4x8 slice.
Arguments:
- pair: bfloat16 [1024, 512, 64], P(('batch', 'dap')), parts along dimension 0
- pair_mask: int32 [1024, 512], P(('batch', 'dap')), parts along dimension 0
- ln_in: bfloat16 [2, 2, 64], replicated
- w_proj: bfloat16 [2, 64, 256], replicated
- b_proj: bfloat16 [2, 256], replicated
- w_gate: bfloat16 [2, 64, 64], replicated
- b_gate: bfloat16 [2, 64], replicated
- ln_out: bfloat16 [2, 2, 64], replicated
- w_out: bfloat16 [2, 64, 64], replicated
- b_out: bfloat16 [2, 64], replicated
Outputs:
- output: bfloat16 [1024, 512, 64], P(('batch', 'dap')), parts along dimension 0
There are 2 independent parts. A program takes and returns all parts, laid end to end along the dimension named above; an argument that names none is the same for every part.
All inputs are finite; a program needn't handle non-finite values.
Results may differ from a plain program's by a relative error of at most 0.00360069.
Values are sent between devices in bfloat16 or wider.
A program may use at most 768 MiB of HBM per device.

v0:
```python
import jax
import jax.numpy as jnp
from jax import lax
from jax.sharding import PartitionSpec as P, NamedSharding

LN_EPS = 1e-5


def norm_last(values, scale, offset):
    centred = values - jnp.mean(values, axis=-1, keepdims=True)
    variance = jnp.mean(centred * centred, axis=-1, keepdims=True)
    return centred * lax.rsqrt(variance + LN_EPS) * scale.astype(jnp.float32) + offset.astype(jnp.float32)


def norm_channels(values, scale, offset):
    centred = values - jnp.mean(values, axis=-3, keepdims=True)
    variance = jnp.mean(centred * centred, axis=-3, keepdims=True)
    return (centred * lax.rsqrt(variance + LN_EPS) * scale.astype(jnp.float32)[:, None, None]
            + offset.astype(jnp.float32)[:, None, None])


def gated_side(projected, keep_mask, channels):
    return (keep_mask * jax.nn.sigmoid(projected[channels:2 * channels]) * projected[:channels]).astype(jnp.bfloat16)


def normalize_project(pair, keep_mask, ln_in, w_proj, b_proj, channels):
    normed = norm_last(pair.astype(jnp.float32), ln_in[0], ln_in[1]).astype(jnp.bfloat16)
    projected = jnp.einsum("zc,ijz->cij", w_proj, normed, preferred_element_type=jnp.float32)
    projected = projected + b_proj.astype(jnp.float32)[:, None, None]
    left = gated_side(projected[:2 * channels], keep_mask, channels)
    right = gated_side(projected[2 * channels:], keep_mask, channels)
    return normed, left, right


def finish_layer(pair, normed, tri_sum, w_gate, b_gate, ln_out, w_out, b_out):
    tri_norm = norm_channels(tri_sum, ln_out[0], ln_out[1]).astype(jnp.bfloat16)
    update = jnp.einsum("cij,cz->ijz", tri_norm, w_out, preferred_element_type=jnp.float32) + b_out.astype(jnp.float32)
    gates = jax.nn.sigmoid(jnp.einsum("ijz,zy->ijy", normed, w_gate, preferred_element_type=jnp.float32) + b_gate.astype(jnp.float32))
    return (pair.astype(jnp.float32) + gates * update).astype(jnp.bfloat16)


def solution(mesh):
    row_spec = P(("batch", "dap"), None, None)
    mask_spec = P(("batch", "dap"), None)

    def local_layers(pair, pair_mask, ln_in, w_proj, b_proj, w_gate, b_gate, ln_out, w_out, b_out):
        channels = w_out.shape[1]
        keep_mask = pair_mask.astype(jnp.float32)[None]
        normed, left, right = normalize_project(pair, keep_mask, ln_in[0], w_proj[0], b_proj[0], channels)
        right_all = lax.all_gather(right, "dap", axis=1, tiled=True)
        tri_sum = jnp.einsum("cik,cjk->cij", left, right_all, preferred_element_type=jnp.float32)
        first = finish_layer(pair, normed, tri_sum, w_gate[0], b_gate[0], ln_out[0], w_out[0], b_out[0])
        normed, left, right = normalize_project(first, keep_mask, ln_in[1], w_proj[1], b_proj[1], channels)
        left_cols = lax.all_to_all(left, "dap", 2, 1, tiled=True)
        right_all = lax.all_gather(right, "dap", axis=1, tiled=True)
        tri_sum = jnp.einsum("cki,ckj->cij", left_cols, right_all, preferred_element_type=jnp.float32)
        return finish_layer(first, normed, tri_sum, w_gate[1], b_gate[1], ln_out[1], w_out[1], b_out[1])

    return jax.shard_map(local_layers, mesh=mesh,
                         in_specs=(row_spec, mask_spec, P(), P(), P(), P(), P(), P(), P(), P()),
                         out_specs=row_spec, check_vma=False)
```

profile of v0, /device:TPU:113, one launch (start us, length us, event | category | flops | bytes accessed | tf_op | source)
XLA Modules:
  0.0 593.7 jit_solution(17337975297099514781)
XLA Ops:
  6.5 0.0 copy-start.8
  6.5 0.0 copy-start.5
  6.6 0.0 copy-start.6
  6.6 0.0 all-gather.3.cloned.1.call-start
  6.6 0.0 copy-start
  6.6 0.9 bitcast_convert_fusion.5
  7.4 3.9 convert_reduce_fusion.1
  11.3 3.9 fusion.12
  15.2 0.0 copy-done.8
  15.2 0.0 copy-done.5
  15.3 0.0 copy-done.6
  15.3 0.0 copy-done
  15.3 13.4 %add_bitcast_fusion.1 = f32[256,64,512]{2,0,1:T(8,128)} fusion(f32[256]{0:T(256)S(1)} %bitcast.85, bf16[2,64,256]{2,1,0:T(8,128)(2,1)S(1)} %copy-done.6, bf16[64,512,64]{1,2,0:T(8,128)(2,1)S(1)} %copy-done, f32[64]{0:T(128)S(1)} %get-tuple-element.14, f32[64]{0:T(128)S(1)} %get-tuple-element.15, f32[64,512]{1,0:T(8,128)S(1)} %add_rsqrt_fusion.3, ...), kind=kOutput, calls=%fused_computation.5 | convolution fusion | flops 1094713344 | bytes 38045696 | tf_op jit(solution)/shard_map/zc,ijz->cij/dot_general | solution.py:28
  28.7 0.0 copy-start.9
  28.7 0.0 copy-start.10
  28.7 0.0 copy-start.11
  28.7 17.1 %fusion.33 = (bf16[64,64,512]{2,0,1:T(8,128)(2,1)}, bf16[64,64,512]{2,0,1:T(8,128)(2,1)}) fusion(f32[256,64,512]{2,0,1:T(8,128)} %add_bitcast_fusion.1, f32[64,512]{1,0:T(8,128)S(1)} %convert_element_type.153), kind=kLoop, calls=%fused_computation.48 | loop fusion | flops 25165824 | bytes 42074112 | tf_op jit(solution)/shard_map/convert_element_type | solution.py:23
  45.8 0.1 all-gather.3.cloned.1.call-update
  45.9 0.5 all-gather.5.cloned.1.call-start
  46.4 0.0 copy-done.9
  46.4 0.0 copy-done.10
  46.4 0.0 copy-done.11
  46.5 155.6 %all-gather.3.cloned.1.call-done = bf16[64,512,512]{2,0,1:T(8,128)(2,1)} async-done(((bf16[64,64,512]{2,0,1:T(8,128)(2,1)}), bf16[64,512,512]{2,0,1:T(8,128)(2,1)}) %all-gather.3.cloned.1.call-update) | async-done | bytes 33554448 | tf_op jit(solution)/shard_map/all_gather | solution.py:50
  202.0 45.4 %fusion.59 = (f32[64,512]{1,0:T(8,128)S(1)}, f32[64,64,512]{2,1,0:T(8,128)}) fusion(bf16[64,512,512]{2,0,1:T(8,128)(2,1)} %all-gather.3.cloned.1.call-done, bf16[64,64,512]{2,0,1:T(8,128)(2,1)} %get-tuple-element.7), kind=kOutput, calls=%fused_computation.97 | convolution fusion | flops 2149548032 | bytes 46268416 | tf_op jit(solution)/shard_map/cik,cjk->cij/dot_general | solution.py:51
  247.4 0.0 copy-start.2
  247.4 4.7 multiply_reduce_fusion.1
  252.1 0.0 copy-start.7
  252.1 1.0 copy-done.2
  253.1 2.2 add_convert_fusion.1
  255.4 0.0 copy-done.7
  255.4 0.0 copy-start.1
  255.4 0.0 copy-start.12
  255.4 5.5 fusion.40
  260.9 0.0 copy-done.1
  260.9 0.0 copy-done.12
  260.9 5.6 convert_reduce_fusion
  266.5 0.0 copy-start.3
  266.5 1.8 fusion.8
  268.4 0.1 copy-done.3
  268.5 13.8 %add_bitcast_fusion = f32[256,64,512]{2,0,1:T(8,128)} fusion(f32[256]{0:T(256)S(1)} %bitcast.84, bf16[2,64,256]{2,1,0:T(8,128)(2,1)S(1)} %copy-done.6, bf16[64,512,64]{1,2,0:T(8,128)(2,1)S(1)} %get-tuple-element.26, f32[64]{0:T(128)S(1)} %get-tuple-element.16, f32[64]{0:T(128)S(1)} %get-tuple-element.13, f32[64,512]{1,0:T(8,128)S(1)} %add_rsqrt_fusion.1, ...), kind=kOutput, calls=%fused_computation.4 | convolution fusion | flops 1094713344 | bytes 38045696 | tf_op jit(solution)/shard_map/zc,ijz->cij/dot_general | solution.py:28
  282.3 17.0 %fusion.18 = (bf16[64,64,512]{2,0,1:T(8,128)(2,1)}, bf16[64,64,512]{2,0,1:T(8,128)(2,1)}) fusion(f32[256,64,512]{2,0,1:T(8,128)} %add_bitcast_fusion, f32[64,512]{1,0:T(8,128)S(1)} %convert_element_type.153), kind=kLoop, calls=%fused_computation.27 | loop fusion | flops 25165824 | bytes 42074112 | tf_op jit(solution)/shard_map/convert_element_type | solution.py:23
  299.3 0.1 all-gather.5.cloned.1.call-update
  299.4 13.0 %copy.27 = bf16[64,64,512]{0,1,2:T(8,128)(2,1)} copy(bf16[64,64,512]{2,0,1:T(8,128)(2,1)} %get-tuple-element.6) | data formatting | bytes 8388608 | tf_op jit(solution)/shard_map/convert_element_type | solution.py:23
  312.4 10.5 %reshape.155 = bf16[8,2,131072]{2,1,0:T(2,128)(2,1)} reshape(bf16[512,64,64]{2,1,0:T(8,128)(2,1)} %bitcast.81) | data formatting | bytes 8388608
  322.9 98.6 %all_to_all.18 = bf16[8,2,131072]{2,1,0:T(2,128)(2,1)} all-to-all(bf16[8,2,131072]{2,1,0:T(2,128)(2,1)} %reshape.155), channel_id=1, replica_groups=mesh['batch'=2,'dap'=8] {'dap'}, dimensions={0} | all-to-all | bytes 8388608 | tf_op jit(solution)/shard_map/all_to_all | solution.py:54
  421.5 10.3 %reshape.156 = bf16[512,64,64]{2,1,0:T(8,128)(2,1)} reshape(bf16[8,2,131072]{2,1,0:T(2,128)(2,1)} %all_to_all.18) | data formatting | bytes 8388608
  431.8 12.5 %copy.28 = bf16[64,64,8,64]{1,2,3,0:T(8,128)(2,1)} copy(bf16[64,64,8,64]{0,1,3,2:T(8,128)(2,1)} %bitcast.82) | data formatting | bytes 8388608 | tf_op jit(solution)/shard_map/all_to_all | solution.py:54
  444.3 11.8 %all_to_all.16 = bf16[64,512,64]{1,2,0:T(8,128)(2,1)} reshape(bf16[64,8,64,64]{2,1,3,0:T(8,128)(2,1)} %bitcast.83) | data formatting | bytes 8388608 | tf_op jit(solution)/shard_map/all_to_all | solution.py:54
  456.1 41.9 %all-gather.5.cloned.1.call-done = bf16[64,512,512]{2,0,1:T(8,128)(2,1)} async-done(((bf16[64,64,512]{2,0,1:T(8,128)(2,1)}), bf16[64,512,512]{2,0,1:T(8,128)(2,1)}) %all-gather.5.cloned.1.call-update) | async-done | bytes 33554448 | tf_op jit(solution)/shard_map/all_gather | solution.py:55
  498.1 73.5 %fusion.60 = (f32[64,512]{1,0:T(8,128)S(1)}, f32[64,64,512]{2,1,0:T(8,128)S(1)}) fusion(bf16[64,512,64]{1,2,0:T(8,128)(2,1)} %all_to_all.16, bf16[64,512,512]{2,0,1:T(8,128)(2,1)} %all-gather.5.cloned.1.call-done), kind=kOutput, calls=%fused_computation.98 | convolution fusion | flops 2149548032 | bytes 46268416 | tf_op jit(solution)/shard_map/cki,ckj->cij/dot_general | solution.py:56
  571.6 1.1 multiply_reduce_fusion
  572.7 2.1 add_convert_fusion
  574.8 0.0 copy-start.4
  574.9 5.5 fusion.38
  580.3 0.0 copy-done.4
  580.3 6.1 %fusion.17 = bf16[64,512,64]{1,2,0:T(8,128)(2,1)} fusion(bf16[64,512,64]{1,2,0:T(8,128)(2,1)S(1)} %copy-done.4, f32[64,512,64]{1,2,0:T(8,128)S(1)} %fusion.38, f32[64]{0:T(128)S(1)} %get-tuple-element.21, f32[64]{0:T(128)S(1)} %get-tuple-element.30, bf16[2,64,64]{2,1,0:T(8,128)(2,1)S(1)} %copy-done.12, f32[64]{0:T(128)S(1)} %get-tuple-element.16, ...), kind=kOutput, calls=%fused_computation.25 | convolution fusion | flops 299892736 | bytes 21252096 | tf_op jit(solution)/shard_map/ijz,zy->ijy/dot_general | solution.py:38
  (12 shorter events, 0.2 us)
Async XLA Ops:
  6.5 8.7 %copy-start.8 = (bf16[2,256]{1,0:T(2,128)(2,1)S(1)}, bf16[2,256]{1,0:T(2,128)(2,1)}, u32[]{:S(2)}) copy-start(bf16[2,256]{1,0:T(2,128)(2,1)} %param.14) | copy-start | bytes 3076
  6.5 8.7 %copy-start.5 = (s32[64,512]{1,0:T(8,128)S(1)}, s32[64,512]{1,0:T(8,128)}, u32[]{:S(2)}) copy-start(s32[64,512]{1,0:T(8,128)} %param.11) | copy-start | bytes 393220
  6.6 8.7 %copy-start.6 = (bf16[2,64,256]{2,1,0:T(8,128)(2,1)S(1)}, bf16[2,64,256]{2,1,0:T(8,128)(2,1)}, u32[]{:S(2)}) copy-start(bf16[2,64,256]{2,1,0:T(8,128)(2,1)} %param.13) | copy-start | bytes 196612
  6.6 195.5 %all-gather.3.cloned.1.call-start = ((), (), s32[]{:S(2)}) async-start(), calls=%async_computation.1 | async-start | bytes 37748736 | tf_op jit(solution)/shard_map/all_gather | solution.py:50
  6.6 8.7 %copy-start = (bf16[64,512,64]{1,2,0:T(8,128)(2,1)S(1)}, bf16[64,512,64]{1,2,0:T(8,128)(2,1)}, u32[]{:S(2)}) copy-start(bf16[64,512,64]{1,2,0:T(8,128)(2,1)} %param.10) | copy-start | bytes 12582916
  28.7 17.7 %copy-start.9 = (bf16[2,2,64]{2,1,0:T(2,128)(2,1)S(1)}, bf16[2,2,64]{2,1,0:T(2,128)(2,1)}, u32[]{:S(2)}) copy-start(bf16[2,2,64]{2,1,0:T(2,128)(2,1)} %param.17) | copy-start | bytes 1540
  28.7 17.7 %copy-start.10 = (bf16[2,64]{1,0:T(2,128)(2,1)S(1)}, bf16[2,64]{1,0:T(2,128)(2,1)}, u32[]{:S(2)}) copy-start(bf16[2,64]{1,0:T(2,128)(2,1)} %param.19) | copy-start | bytes 772
  28.7 17.7 %copy-start.11 = (bf16[2,64]{1,0:T(2,128)(2,1)S(1)}, bf16[2,64]{1,0:T(2,128)(2,1)}, u32[]{:S(2)}) copy-start(bf16[2,64]{1,0:T(2,128)(2,1)} %param.16) | copy-start | bytes 772
  45.9 452.2 %all-gather.5.cloned.1.call-start = ((), (), s32[]{:S(2)}) async-start(), calls=%async_computation.2 | async-start | bytes 37748736 | tf_op jit(solution)/shard_map/all_gather | solution.py:55
  247.4 5.8 copy-start.2
  252.1 3.3 copy-start.7
  255.4 5.5 copy-start.1
  255.4 5.5 copy-start.12
  266.5 2.0 copy-start.3
  574.8 5.5 copy-start.4
Sparse Core Ops, SparseCore 0:
  46.0 155.9 all-gather.2
  299.5 198.5 all-gather.4
where the time goes:
time: 602 us; the launch traced here: 594 us
  waiting for transfers between devices  198 us (33%)
  matrix products  169 us (28%)
  blocking collectives  98.6 us (16%)
  local copies, waits for them, and re-layouts  59.3 us (10%)
  other arithmetic  54.8 us (9%)
  between operations  14.1 us (2%)
    all_gather x2, waiting for transfers between devices, local_layers(): right_all = lax.all_gather(right, 'dap', axis=1, tiled=True)  197 us
    all_to_all x1, blocking collectives, local_layers(): left_cols = lax.all_to_all(left, 'dap', 2, 1, tiled=True)  98.6 us
    dot_general x1, matrix products, local_layers(): jnp.einsum('cki,ckj->cij', left_cols, right_all, preferred_element_type=j...  73.5 us
    dot_general x1, matrix products, local_layers(): jnp.einsum('cik,cjk->cij', left, right_all, preferred_element_type=jnp.fl...  45.4 us
    convert_element_type x2, other arithmetic, gated_side(): (keep_mask * jax.nn.sigmoid(projected[channels:2 * channels]) * projected...  34.1 us
    dot_general x2, matrix products, normalize_project(): jnp.einsum('zc,ijz->cij', w_proj, normed, preferred_element_type=jnp.floa...  27.2 us
    all_to_all x2, local copies, waits for them, and re-layouts, local_layers(): left_cols = lax.all_to_all(left, 'dap', 2, 1, tiled=True)  24.3 us
    unnamed x28, local copies, waits for them, and re-layouts  22 us
  transfers between devices with their start and end apart: 2, of which 2 were waited for; matrix products, arithmetic and copies ran while one was open for 8% of the time, Pallas kernels for 0%

commit v1 on v0

v1 whole, which is shorter than its diff:
```python
import functools

import jax
import jax.numpy as jnp
from jax import lax
from jax.experimental import pallas as pl
from jax.experimental.pallas import tpu as pltpu
from jax.sharding import PartitionSpec as P

LN_EPS = 1e-5
F32 = jnp.float32
BF16 = jnp.bfloat16
VMEM_LIMIT = 60 * 1024 * 1024
LANES = 256


def cost(flops, nbytes):
    return pl.CostEstimate(flops=flops, bytes_accessed=nbytes, transcendentals=0)


def norm_rows(x, scale, offset):
    inv = 1.0 / x.shape[0]
    centred = x - jnp.sum(x, axis=0, keepdims=True) * inv
    variance = jnp.sum(centred * centred, axis=0, keepdims=True) * inv
    return centred * lax.rsqrt(variance + LN_EPS) * scale + offset


def gated_pair(low, high, w_ref, bias_ref, side):
    def half(zn, order):
        value = jnp.dot(w_ref[order, 2 * side], zn, preferred_element_type=F32)
        gate = jnp.dot(w_ref[order, 2 * side + 1], zn, preferred_element_type=F32)
        reps = zn.shape[1] // 128
        value = value + jnp.concatenate([bias_ref[order, 2 * side]] * reps, axis=1)
        gate = gate + jnp.concatenate([bias_ref[order, 2 * side + 1]] * reps, axis=1)
        out = (jnp.tanh(gate) + 1.0) * value
        return out.reshape(out.shape[0] // 8, 8, out.shape[1])

    first = half(low, 0)
    second = half(high, 1)
    upper = lax.broadcasted_iota(jnp.int32, first.shape, 1) < 4
    return jnp.where(upper, first, second), jnp.where(upper, second, first)


def sides_kernel(g, info, z_ref, m_ref, w_ref, bias_ref, ln_ref, *rest):
    a_ref, b_ref, zn_ref, zh_ref, scr = rest[-5:]
    dev = pl.program_id(0)
    mine = lax.rem(dev, 2) == info[1]
    rows, chans, cols = scr.shape

    for r in range(rows):
        for l in range(0, cols, LANES):
            x = z_ref[0, r, :, l:l + LANES].astype(F32)
            scr[r, :, l:l + LANES] = norm_rows(x, ln_ref[0], ln_ref[1]).astype(BF16)

    def emit(out_ref, side):
        for l in range(0, cols, LANES):
            even, odd = [], []
            for h in range(0, rows, 8):
                low = scr[h:h + 4, :, l:l + LANES].reshape(4 * chans, LANES)
                high = scr[h + 4:h + 8, :, l:l + LANES].reshape(4 * chans, LANES)
                e, o = gated_pair(low, high, w_ref, bias_ref, side)
                mask = m_ref[h:h + 8, l:l + LANES].astype(F32)
                even.append(e * mask[None])
                odd.append(pltpu.roll(o, 4, 1) * mask[None])
            out_ref[:, 0, :, l:l + LANES] = jnp.concatenate(even, axis=1).astype(BF16)
            out_ref[:, 1, :, l:l + LANES] = jnp.concatenate(odd, axis=1).astype(BF16)

    emit(b_ref, 1)

    @pl.when(mine)
    def _():
        emit(a_ref, 0)
        zn_ref[...] = scr[...]
        zh_ref[...] = z_ref[0]


def sides_call(g, chunks, info, zg, mask, w4, bias4, ln, prev):
    devs, rows, chans, cols = zg.shape
    per = chunks
    shapes = [jax.ShapeDtypeStruct((chans // 2, 2, devs // 2 * per * rows, cols), BF16),
              jax.ShapeDtypeStruct((chans // 2, 2, devs * per * rows, cols), BF16),
              jax.ShapeDtypeStruct((devs // 2 * per * rows, chans, cols), BF16),
              jax.ShapeDtypeStruct((devs // 2 * per * rows, chans, cols), BF16)]
    full = lambda arr: pl.BlockSpec(arr.shape, lambda i, info: (0,) * arr.ndim)
    in_specs = [pl.BlockSpec((1, rows, chans, cols), lambda i, info: (i, 0, 0, 0)),
                pl.BlockSpec((rows, cols), lambda i, info: (i * per + g, 0)),
                full(w4), full(bias4), full(ln)]
    args = [zg, mask, w4, bias4, ln]
    aliases = {}
    if prev is not None:
        in_specs += [pl.BlockSpec(memory_space=pl.ANY)] * 4
        aliases = {1 + len(args) + n: n for n in range(4)}
        args += list(prev)
    half_row = lambda i, info: (lax.div(i, 2) * per + g, 0, 0)
    out_specs = [pl.BlockSpec((chans // 2, 2, rows, cols), lambda i, info: (0, 0, lax.div(i, 2) * per + g, 0)),
                 pl.BlockSpec((chans // 2, 2, rows, cols), lambda i, info: (0, 0, i * per + g, 0)),
                 pl.BlockSpec((rows, chans, cols), half_row),
                 pl.BlockSpec((rows, chans, cols), half_row)]
    return pl.pallas_call(
        functools.partial(sides_kernel, g),
        out_shape=shapes,
        grid_spec=pltpu.PrefetchScalarGridSpec(
            num_scalar_prefetch=1, grid=(devs,), in_specs=in_specs, out_specs=out_specs,
            scratch_shapes=[pltpu.VMEM((rows, chans, cols), BF16)]),
        input_output_aliases=aliases,
        compiler_params=pltpu.CompilerParams(vmem_limit_bytes=VMEM_LIMIT, dimension_semantics=("arbitrary",)),
        cost_estimate=cost(12_000_000_000, 40_000_000),
        name=f"sides_{g}",
    )(info, *args)


def finish_rows(v, zn, z, ln_ref, wo_ref, bo_ref, wg_ref, bg_ref):
    chans, rows, n = v.shape
    inv = 1.0 / chans
    reps = n // 128
    wide = lambda ref, k: jnp.concatenate([ref[k]] * reps, axis=-1)
    mean = jnp.sum(v, axis=0) * inv
    centred = v - mean[None]
    variance = jnp.sum(centred * centred, axis=0) * inv
    normed = centred * lax.rsqrt(variance + LN_EPS)[None]
    normed = normed * wide(ln_ref, 0) + wide(ln_ref, 1)
    u = normed.reshape(chans * rows, n).astype(BF16)
    update = jnp.dot(wo_ref[...], u, preferred_element_type=F32) + jnp.concatenate([bo_ref[...]] * reps, axis=1)
    k = wg_ref.shape[0]
    zn2 = zn.reshape(rows * chans, n)
    gate = jnp.concatenate([jnp.dot(wg_ref[...], zn2[q:q + k], preferred_element_type=F32)
                            for q in range(0, rows * chans, k)], axis=0)
    gate = jnp.tanh(gate + jnp.concatenate([bg_ref[...]] * reps, axis=1)) + 1.0
    out = z.astype(F32).reshape(rows * chans, n) + gate * update
    return out.astype(BF16).reshape(rows, chans, n)


def first_kernel(a_ref, b_ref, zn_ref, z_ref, ln_ref, wo_ref, bo_ref, wg_ref, bg_ref, out_ref, o_scr):
    t, s = pl.program_id(0), pl.program_id(1)
    per = a_ref.shape[0]

    @pl.when(t < 2)
    def _():
        for q in range(per):
            o_scr[lax.rem(t, 2), s * per + q] = lax.dot_general(
                a_ref[q], b_ref[q], (((1,), (1,)), ((), ())), preferred_element_type=F32)

    @pl.when(t > 0)
    def _():
        rows = out_ref.shape[0]

        @pl.loop(0, rows, step=8)
        def _(r):
            start = pl.multiple_of(s * rows + r, 8)
            v = o_scr[lax.rem(t + 1, 2), :, pl.ds(start, 8), :]
            out_ref[pl.ds(r, 8)] = finish_rows(v, zn_ref[pl.ds(r, 8)], z_ref[pl.ds(r, 8)],
                                               ln_ref, wo_ref, bo_ref, wg_ref, bg_ref)


def first_call(a, b, zn, zh, fin):
    chans, rows, cols = a.shape
    steps = 8
    per = chans // steps
    tile = LANES
    ntile = b.shape[1] // tile
    assert ntile == 2
    rstep = rows // steps
    full = lambda arr: pl.BlockSpec(arr.shape, lambda t, s: (0,) * arr.ndim)
    last = steps - 1
    row_map = lambda t, s: (jnp.where(t > 0, s, 0), 0, jnp.maximum(t - 1, 0))
    return pl.pallas_call(
        first_kernel,
        out_shape=jax.ShapeDtypeStruct(zh.shape, BF16),
        grid=(ntile + 1, steps),
        in_specs=[pl.BlockSpec((per, rows, cols), lambda t, s: (jnp.where(t < 2, s, last), 0, 0)),
                  pl.BlockSpec((per, tile, cols), lambda t, s: (jnp.where(t < 2, s, last), jnp.minimum(t, 1), 0)),
                  pl.BlockSpec((rstep, zn.shape[1], tile), row_map),
                  pl.BlockSpec((rstep, zn.shape[1], tile), row_map)] + [full(f) for f in fin],
        out_specs=pl.BlockSpec((rstep, zn.shape[1], tile), row_map),
        scratch_shapes=[pltpu.VMEM((2, chans, rows, tile), F32)],
        compiler_params=pltpu.CompilerParams(vmem_limit_bytes=VMEM_LIMIT,
                                             dimension_semantics=("arbitrary", "arbitrary")),
        cost_estimate=cost(40_000_000_000, 140_000_000),
        name="first_layer",
    )(a, b, zn, zh, *fin)


def second_sides_kernel(info, z_ref, m_ref, w_ref, bias_ref, ln_ref, a_ref, b_ref, scr):
    rows, chans, cols = scr.shape
    for r in range(rows):
        for l in range(0, cols, LANES):
            x = z_ref[r, :, l:l + LANES].astype(F32)
            scr[r, :, l:l + LANES] = norm_rows(x, ln_ref[0], ln_ref[1]).astype(BF16)

    def emit(out_ref, side, width, start, out_start):
        even, odd = [], []
        for h in range(0, rows, 8):
            low = scr[h:h + 4, :, pl.ds(start, width)].reshape(4 * chans, width)
            high = scr[h + 4:h + 8, :, pl.ds(start, width)].reshape(4 * chans, width)
            e, o = gated_pair(low, high, w_ref, bias_ref, side)
            mask = m_ref[h:h + 8, pl.ds(start, width)].astype(F32)
            even.append(e * mask[None])
            odd.append(o * pltpu.roll(mask, 4, 0)[None])
        out_ref[:, 0, :, out_start:out_start + width] = jnp.concatenate(even, axis=1).astype(BF16)
        out_ref[:, 1, :, out_start:out_start + width] = jnp.concatenate(odd, axis=1).astype(BF16)

    for l in range(0, cols, LANES):
        emit(b_ref, 1, LANES, l, l)
    width = a_ref.shape[3]
    emit(a_ref, 0, width, pl.multiple_of(info[0] * width, width), 0)


def second_sides_call(info, z1, mask, w4, bias4, ln, width, per):
    nrow, chans, cols = z1.shape
    rows = 16
    full = lambda arr: pl.BlockSpec(arr.shape, lambda i, info: (0,) * arr.ndim)
    mask_map = lambda i, info: ((2 * lax.div(i, per) + info[1]) * per + lax.rem(i, per), 0)
    return pl.pallas_call(
        second_sides_kernel,
        out_shape=[jax.ShapeDtypeStruct((chans // 2, 2, nrow, width), BF16),
                   jax.ShapeDtypeStruct((chans // 2, 2, nrow, cols), BF16)],
        grid_spec=pltpu.PrefetchScalarGridSpec(
            num_scalar_prefetch=1, grid=(nrow // rows,),
            in_specs=[pl.BlockSpec((rows, chans, cols), lambda i, info: (i, 0, 0)),
                      pl.BlockSpec((rows, cols), mask_map), full(w4), full(bias4), full(ln)],
            out_specs=[pl.BlockSpec((chans // 2, 2, rows, width), lambda i, info: (0, 0, i, 0)),
                       pl.BlockSpec((chans // 2, 2, rows, cols), lambda i, info: (0, 0, i, 0))],
            scratch_shapes=[pltpu.VMEM((rows, chans, cols), BF16)]),
        compiler_params=pltpu.CompilerParams(vmem_limit_bytes=VMEM_LIMIT, dimension_semantics=("arbitrary",)),
        cost_estimate=cost(12_000_000_000, 40_000_000),
        name="second_sides",
    )(info, z1, mask, w4, bias4, ln)


def partial_kernel(info, a_ref, b_ref, keep_ref, send_ref):
    half = keep_ref.shape[1]

    def run(own, other):
        for q in range(a_ref.shape[0]):
            total = lax.dot_general(a_ref[q], b_ref[q], (((0,), (0,)), ((), ())), preferred_element_type=F32)
            own[q] = total[:half]
            other[q] = total[half:]

    @pl.when(info[1] == 0)
    def _():
        run(keep_ref, send_ref)

    @pl.when(info[1] == 1)
    def _():
        run(send_ref, keep_ref)


def partial_call(info, a, b, part, parts):
    chans, rows, width = a.shape
    cols = b.shape[2] // parts
    per = 8
    out = jax.ShapeDtypeStruct((chans, width // 2, cols), F32)
    return pl.pallas_call(
        partial_kernel,
        out_shape=[out, out],
        grid_spec=pltpu.PrefetchScalarGridSpec(
            num_scalar_prefetch=1, grid=(chans // per,),
            in_specs=[pl.BlockSpec((per, rows, width), lambda i, info: (i, 0, 0)),
                      pl.BlockSpec((per, rows, cols), lambda i, info: (i, 0, part))],
            out_specs=[pl.BlockSpec((per, width // 2, cols), lambda i, info: (i, 0, 0))] * 2),
        compiler_params=pltpu.CompilerParams(vmem_limit_bytes=VMEM_LIMIT, dimension_semantics=("arbitrary",)),
        cost_estimate=cost(5_000_000_000, 20_000_000),
        name=f"partial_{part}",
    )(info, a, b)


def second_kernel(info, own_ref, got_ref, z_ref, lni_ref, ln_ref, wo_ref, bo_ref, wg_ref, bg_ref, *rest):
    out_ref, scr = rest[-2:]
    rows, chans, n = scr.shape
    for r in range(rows):
        scr[r] = norm_rows(z_ref[r].astype(F32), lni_ref[0], lni_ref[1]).astype(BF16)
    for r in range(0, rows, 8):
        v = own_ref[:, r:r + 8, :] + got_ref[:, r:r + 8, :]
        out_ref[r:r + 8] = finish_rows(v, scr[r:r + 8], z_ref[r:r + 8], ln_ref, wo_ref, bo_ref, wg_ref, bg_ref)


def second_call(info, own, got, z1, lni, fin, part, prev):
    chans, nrow, n = own.shape
    rows = 16
    full = lambda arr: pl.BlockSpec(arr.shape, lambda i, info: (0,) * arr.ndim)
    steps = nrow // rows
    args = [own, got, z1, lni] + list(fin)
    in_specs = [pl.BlockSpec((chans, rows, n), lambda i, info: (0, i, 0)),
                pl.BlockSpec((chans, rows, n), lambda i, info: (0, i, 0)),
                pl.BlockSpec((rows, chans, n), lambda i, info: (info[0] * steps + i, 0, part)),
                full(lni)] + [full(f) for f in fin]
    aliases = {}
    if prev is not None:
        aliases = {1 + len(args): 0}
        args.append(prev)
        in_specs.append(pl.BlockSpec(memory_space=pl.ANY))
    return pl.pallas_call(
        second_kernel,
        out_shape=jax.ShapeDtypeStruct((nrow, chans, z1.shape[2]), BF16),
        grid_spec=pltpu.PrefetchScalarGridSpec(
            num_scalar_prefetch=1, grid=(steps,), in_specs=in_specs,
            out_specs=pl.BlockSpec((rows, chans, n), lambda i, info: (i, 0, part)),
            scratch_shapes=[pltpu.VMEM((rows, chans, n), BF16)]),
        input_output_aliases=aliases,
        compiler_params=pltpu.CompilerParams(vmem_limit_bytes=VMEM_LIMIT, dimension_semantics=("arbitrary",)),
        cost_estimate=cost(5_000_000_000, 20_000_000),
        name=f"second_layer_{part}",
    )(info, *args)


def side_weights(w_proj, b_proj, chans):
    wt = (0.5 * w_proj.astype(F32)).T.reshape(4, chans, -1)
    bias = (0.5 * b_proj.astype(F32)).reshape(4, chans)
    swap = lambda x: x.reshape((4, chans // 2, 2) + x.shape[2:])[:, :, ::-1].reshape(x.shape)
    eye = jnp.eye(4, dtype=F32)
    spread = lambda x: (x[:, :, None, None, :] * eye[None, None, :, :, None]).reshape(4, 4 * chans, -1)
    w4 = jnp.stack([spread(wt), spread(swap(wt))]).astype(BF16)
    rep = lambda x: jnp.broadcast_to(x[:, :, None, None], (4, chans, 4, 128)).reshape(4, 4 * chans, 128)
    return w4, jnp.stack([rep(bias), rep(swap(bias))])


def finish_weights(ln_out, w_out, b_out, w_gate, b_gate):
    chans = w_out.shape[0]
    ln = jnp.broadcast_to(ln_out.astype(F32)[:, :, None, None], (2, chans, 8, 128))
    eye8 = jnp.eye(8, dtype=F32)
    wo = 0.5 * w_out.astype(F32)
    wo = (wo.T[None, :, :, None] * eye8[:, None, None, :]).reshape(8 * wo.shape[1], chans * 8).astype(BF16)
    bo = jnp.broadcast_to((0.5 * b_out.astype(F32))[None, :, None], (8, chans, 128)).reshape(8 * chans, 128)
    eye4 = jnp.eye(4, dtype=F32)
    wg = 0.5 * w_gate.astype(F32)
    wg = (wg.T[None, :, None, :] * eye4[:, None, :, None]).reshape(4 * chans, 4 * chans).astype(BF16)
    bg = jnp.broadcast_to((0.5 * b_gate.astype(F32))[None, :, None], (8, chans, 128)).reshape(8 * chans, 128)
    return ln, wo, bo, wg, bg


def in_norm(ln_in, width):
    return jnp.broadcast_to(ln_in.astype(F32)[:, :, None], (2, ln_in.shape[1], width))


def solution(mesh):
    row_spec = P(("batch", "dap"), None, None)
    mask_spec = P(("batch", "dap"), None)
    devs = mesh.shape["dap"]

    def local_layers(pair, pair_mask, ln_in, w_proj, b_proj, w_gate, b_gate, ln_out, w_out, b_out):
        nrow, cols, chans = pair.shape
        me = lax.axis_index("dap")
        info = jnp.stack([lax.div(me, 2), lax.rem(me, 2)]).astype(jnp.int32)
        zt = pair.transpose(0, 2, 1)
        rows = 16
        chunks = nrow // rows
        mask = lax.all_gather(pair_mask, "dap", axis=0, tiled=True)
        w4, bias4 = side_weights(w_proj[0], b_proj[0], chans)
        w4b, bias4b = side_weights(w_proj[1], b_proj[1], chans)
        lni = in_norm(ln_in[0], LANES)
        lnib = in_norm(ln_in[1], LANES)
        fin = finish_weights(ln_out[0], w_out[0], b_out[0], w_gate[0], b_gate[0])
        finb = finish_weights(ln_out[1], w_out[1], b_out[1], w_gate[1], b_gate[1])
        parts = None
        for g in range(chunks):
            zg = lax.all_gather(zt[g * rows:(g + 1) * rows], "dap", axis=0, tiled=False)
            parts = sides_call(g, chunks, info, zg, mask, w4, bias4, lni, parts)
        a, b, zn, zh = parts
        merge = lambda x: x.reshape((chans,) + x.shape[2:])
        z1 = first_call(merge(a), merge(b), zn, zh, fin)
        width = 2 * nrow
        a2, b2 = second_sides_call(info, z1, mask, w4b, bias4b, lnib, width, chunks)
        a2, b2 = merge(a2), merge(b2)
        pairs = [(d, d + 1 - 2 * (d % 2)) for d in range(devs)]
        out = None
        nparts = cols // LANES
        sums = []
        for p in range(nparts):
            own, send = partial_call(info, a2, b2, p, nparts)
            sums.append((own, lax.ppermute(send, "dap", pairs)))
        for p, (own, got) in enumerate(sums):
            out = second_call(info, own, got, z1, lnib, finb, p, out)
        return out.transpose(0, 2, 1)

    return jax.shard_map(local_layers, mesh=mesh,
                         in_specs=(row_spec, mask_spec, P(), P(), P(), P(), P(), P(), P(), P()),
                         out_specs=row_spec, check_vma=False)
```

time: 602 us -> 397 us (0.66); the launches traced: 594 us -> 396 us
  Pallas kernels: 0 us -> 227 us
  matrix products: 169 us -> 0 us
  blocking collectives: 98.6 us -> 0 us
  waiting for transfers between devices: 198 us -> 102 us
  other arithmetic: 54.8 us -> 14.9 us
  local copies, waits for them, and re-layouts: 59.3 us -> 37.4 us
    pallas_call x0 -> x10, Pallas kernels: none -> 227 us  [the longest x4 90.5 us: sides_call(): pl.pallas_call(functools.partial(sides_kernel, g), out_shape=shapes, grid...]
    dot_general x8 -> x0, matrix products: 169 us -> none  [the longest x1 73.5 us: local_layers(): jnp.einsum('cki,ckj->cij', left_cols, right_all, preferred_element_type=j...]
    all_to_all x1 -> x0, blocking collectives: 98.6 us -> none  [local_layers(): left_cols = lax.all_to_all(left, 'dap', 2, 1, tiled=True)]
    all_gather x2 -> x5, waiting for transfers between devices: 197 us -> 99 us  [the longest x4 99 us: local_layers(): zg = lax.all_gather(zt[g * rows:(g + 1) * rows], 'dap', axis=0, tiled=False)]
    convert_element_type x8 -> x6, other arithmetic: 38.4 us -> 3.62 us  [the longest x1 1.99 us: finish_weights(): (wo.T[None, :, :, None] * eye8[:, None, None, :]).reshape(8 * wo.shape[1]...]
    all_to_all x2 -> x0, local copies, waits for them, and re-layouts: 24.3 us -> none  [local_layers(): left_cols = lax.all_to_all(left, 'dap', 2, 1, tiled=True)]
    unnamed x28, local copies, waits for them, and re-layouts: 22 us -> 0.28 us
    reduce_sum x5 -> x0, other arithmetic: 15.4 us -> none  [the longest x2 5.84 us: norm_channels(): variance = jnp.mean(centred * centred, axis=-3, keepdims=True)]
  transfers between devices with their start and end apart: 2 -> 7, of which waited for: 2 -> 4; matrix products, arithmetic and copies ran while one was open for 8% -> 12% of each run, Pallas kernels for 0% -> 22%
where the time goes in v1:
time: 397 us; the launch traced here: 396 us
  Pallas kernels  227 us (57%)
  waiting for transfers between devices  102 us (26%)
  local copies, waits for them, and re-layouts  37.4 us (9%)
  other arithmetic  14.9 us (4%)
  between operations  13.4 us (3%)
    all_gather x4, waiting for transfers between devices, local_layers(): zg = lax.all_gather(zt[g * rows:(g + 1) * rows], 'dap', axis=0, tiled=False)  99 us
    pallas_call x4, Pallas kernels, sides_call(): pl.pallas_call(functools.partial(sides_kernel, g), out_shape=shapes, grid...  90.5 us
    pallas_call x1, Pallas kernels, first_call(): pl.pallas_call(first_kernel, out_shape=jax.ShapeDtypeStruct(zh.shape, BF1...  61 us
    pallas_call x1, Pallas kernels, second_sides_call(): pl.pallas_call(second_sides_kernel, out_shape=[jax.ShapeDtypeStruct((chan...  34.4 us
    pallas_call x2, Pallas kernels, partial_call(): pl.pallas_call(partial_kernel, out_shape=[out, out], grid_spec=pltpu.Pref...  23.1 us
    pallas_call x2, Pallas kernels, second_call(): pl.pallas_call(second_kernel, out_shape=jax.ShapeDtypeStruct((nrow, chans...  18.5 us
    mul x10, local copies, waits for them, and re-layouts, side_weights(): x[:, :, None, None, :] * eye[None, None, :, :, None]  10.9 us
  transfers between devices with their start and end apart: 7, of which 4 were waited for; matrix products, arithmetic and copies ran while one was open for 12% of the time, Pallas kernels for 22%

profile of v1, /device:TPU:113, one launch (start us, length us, event | category | flops | bytes accessed | tf_op | source)
XLA Modules:
  0.0 395.6 jit_solution(851980304769042858)
XLA Ops:
  6.6 0.7 all-gather.10.cloned.1.call-update
  7.4 4.3 %fusion.2 = (bf16[16,64,512]{2,1,0:T(8,128)(2,1)}, bf16[16,64,512]{2,1,0:T(8,128)(2,1)}, bf16[16,64,512]{2,1,0:T(8,128)(2,1)}, bf16[16,64,512]{2,1,0:T(8,128)(2,1)}) fusion(bf16[64,64,512]{2,1,0:T(8,128)(2,1)} %bitcast.83), kind=kLoop, calls=%fused_computation.37 | loop fusion | bytes 8388608 | tf_op jit(solution)/shard_map/slice | solution.py:356
  11.8 0.7 all-gather.16.cloned.1.call-update
  12.6 0.6 all-gather.14.cloned.1.call-update
  13.2 0.6 all-gather.12.cloned.1.call-update
  14.0 0.3 rev.12
  14.3 0.3 mul.280
  14.5 1.1 mul.281
  15.8 0.3 rev.14
  16.1 0.3 mul.306
  16.4 2.1 mul.307
  18.5 0.3 mul.273
  18.8 2.1 mul.274
  20.9 0.3 mul.302
  21.2 2.1 mul.303
  23.3 0.9 mul.275
  24.2 1.4 mul.276
  25.6 0.6 multiply_reduce_fusion
  26.9 0.8 mul.284
  27.9 0.7 multiply_bitcast_fusion
  28.8 1.1 multiply_convert_fusion.6
  29.9 1.8 convert_element_type.196.wg_ref
  31.7 0.7 multiply_bitcast_fusion.1
  32.5 2.0 multiply_convert_fusion
  34.4 2.6 convert_element_type.192
  37.0 2.1 copy.59.wo_ref
  39.1 1.3 multiply_bitcast_fusion.5
  40.4 0.7 broadcast_in_dim.126
  41.1 1.2 multiply_bitcast_fusion.4
  42.3 0.7 broadcast_in_dim.129
  43.6 0.8 mul.310
  44.6 0.6 pad_add_fusion.info
  45.2 1.6 multiply_convert_fusion.3
  46.9 1.1 pad_maximum_fusion.w_ref
  48.4 1.1 pad_maximum_fusion.1.bias_ref
  49.5 1.1 pad_maximum_fusion.2.w_ref
  51.0 1.1 pad_maximum_fusion.3.bias_ref
  52.0 0.5 bitcast_convert_fusion
  52.6 25.8 %all-gather.18.cloned.1.call-done = bf16[128,64,512]{2,1,0:T(8,128)(2,1)} async-done(((bf16[16,64,512]{2,1,0:T(8,128)(2,1)}), bf16[128,64,512]{2,1,0:T(8,128)(2,1)}) %all-gather.18.cloned.1.call-update) | async-done | bytes 8388624 | tf_op jit(solution)/shard_map/all_gather | solution.py:356
  78.3 0.7 broadcast_in_dim.123.ln_ref
  79.1 22.7 %sides_0.1 = (bf16[32,2,256,512]{3,2,1,0:T(8,128)(2,1)}, bf16[32,2,512,512]{3,2,1,0:T(8,128)(2,1)}, bf16[256,64,512]{2,1,0:T(8,128)(2,1)}, bf16[256,64,512]{2,1,0:T(8,128)(2,1)}) custom-call(s32[2]{0:T(128)} %pad_add_fusion.info, bf16[8,16,64,512]{3,2,1,0:T(8,128)(2,1)} %bitcast.92, s32[512,512]{1,0:T(8,128)} %all-gather.10.cloned.1.call-done.m_ref, ...), custom_call_target="tpu_custom_call" | custom-call | flops 12000000000 | bytes 40000000 | tf_op jit(solution)/shard_map/sides_0/pallas_call | solution.py:99
  101.8 23.8 %all-gather.16.cloned.1.call-done = bf16[128,64,512]{2,1,0:T(8,128)(2,1)} async-done(((bf16[16,64,512]{2,1,0:T(8,128)(2,1)}), bf16[128,64,512]{2,1,0:T(8,128)(2,1)}) %all-gather.16.cloned.1.call-update) | async-done | bytes 8388624 | tf_op jit(solution)/shard_map/all_gather | solution.py:356
  125.6 22.4 %sides_1.1 = (bf16[32,2,256,512]{3,2,1,0:T(8,128)(2,1)}, bf16[32,2,512,512]{3,2,1,0:T(8,128)(2,1)}, bf16[256,64,512]{2,1,0:T(8,128)(2,1)}, bf16[256,64,512]{2,1,0:T(8,128)(2,1)}) custom-call(s32[2]{0:T(128)} %pad_add_fusion.info, bf16[8,16,64,512]{3,2,1,0:T(8,128)(2,1)} %bitcast.82, ...), custom_call_target="tpu_custom_call", output_to_operand_aliasing={{0}: (6, {}), {1}: (7, {}), {2}: (8, {}), {3}: (9, {})} | custom-call | flops 12000000000 | bytes 40000000 | tf_op jit(solution)/shard_map/sides_1/pallas_call | solution.py:99
  148.0 24.7 %all-gather.14.cloned.1.call-done = bf16[128,64,512]{2,1,0:T(8,128)(2,1)} async-done(((bf16[16,64,512]{2,1,0:T(8,128)(2,1)}), bf16[128,64,512]{2,1,0:T(8,128)(2,1)}) %all-gather.14.cloned.1.call-update) | async-done | bytes 8388624 | tf_op jit(solution)/shard_map/all_gather | solution.py:356
  172.8 22.5 %sides_2.1 = (bf16[32,2,256,512]{3,2,1,0:T(8,128)(2,1)}, bf16[32,2,512,512]{3,2,1,0:T(8,128)(2,1)}, bf16[256,64,512]{2,1,0:T(8,128)(2,1)}, bf16[256,64,512]{2,1,0:T(8,128)(2,1)}) custom-call(s32[2]{0:T(128)} %pad_add_fusion.info, bf16[8,16,64,512]{3,2,1,0:T(8,128)(2,1)} %bitcast.81, ...), custom_call_target="tpu_custom_call", output_to_operand_aliasing={{0}: (6, {}), {1}: (7, {}), {2}: (8, {}), {3}: (9, {})} | custom-call | flops 12000000000 | bytes 40000000 | tf_op jit(solution)/shard_map/sides_2/pallas_call | solution.py:99
  195.2 24.7 %all-gather.12.cloned.1.call-done = bf16[128,64,512]{2,1,0:T(8,128)(2,1)} async-done(((bf16[16,64,512]{2,1,0:T(8,128)(2,1)}), bf16[128,64,512]{2,1,0:T(8,128)(2,1)}) %all-gather.12.cloned.1.call-update) | async-done | bytes 8388624 | tf_op jit(solution)/shard_map/all_gather | solution.py:356
  219.9 22.9 %sides_3.1 = (bf16[32,2,256,512]{3,2,1,0:T(8,128)(2,1)}, bf16[32,2,512,512]{3,2,1,0:T(8,128)(2,1)}, bf16[256,64,512]{2,1,0:T(8,128)(2,1)}, bf16[256,64,512]{2,1,0:T(8,128)(2,1)}) custom-call(s32[2]{0:T(128)} %pad_add_fusion.info, bf16[8,16,64,512]{3,2,1,0:T(8,128)(2,1)} %bitcast.80, ...), custom_call_target="tpu_custom_call", output_to_operand_aliasing={{0}: (6, {}), {1}: (7, {}), {2}: (8, {}), {3}: (9, {})} | custom-call | flops 12000000000 | bytes 40000000 | tf_op jit(solution)/shard_map/sides_3/pallas_call | solution.py:99
  242.8 1.0 broadcast_in_dim.124.ln_ref
  243.8 0.8 broadcast_in_dim.127.bo_ref
  244.6 0.8 broadcast_in_dim.130.bg_ref
  245.5 61.0 %first_layer.1.z_ref = bf16[256,64,512]{2,1,0:T(8,128)(2,1)} custom-call(bf16[64,256,512]{2,1,0:T(8,128)(2,1)} %bitcast.75, bf16[64,512,512]{2,1,0:T(8,128)(2,1)} %bitcast.74, bf16[256,64,512]{2,1,0:T(8,128)(2,1)} %get-tuple-element.41.zn_ref, bf16[256,64,512]{2,1,0:T(8,128)(2,1)} %get-tuple-element.42.z_ref, f32[2,64,8,128]{3,2,1,0:T(8,128)} %broadcast_in_dim.124.ln_ref, ...), custom_call_target="tpu_custom_call" | custom-call | flops 40000000000 | bytes 140000000 | tf_op jit(solution)/shard_map/first_layer/pallas_call | solution.py:166
  306.5 0.7 broadcast_in_dim.138.ln_ref.lni_ref
  307.2 34.4 %second_sides.1 = (bf16[32,2,256,128]{3,2,1,0:T(8,128)(2,1)}, bf16[32,2,256,512]{3,2,1,0:T(8,128)(2,1)}) custom-call(s32[2]{0:T(128)} %pad_add_fusion.info, bf16[256,64,512]{2,1,0:T(8,128)(2,1)} %first_layer.1.z_ref, s32[512,512]{1,0:T(8,128)} %all-gather.10.cloned.1.call-done.m_ref, bf16[2,4,256,256]{3,2,1,0:T(8,128)(2,1)} %pad_maximum_fusion.2.w_ref, ...), custom_call_target="tpu_custom_call" | custom-call | flops 12000000000 | bytes 40000000 | tf_op jit(solution)/shard_map/second_sides/pallas_call | solution.py:213
  341.6 11.5 %partial_0.1 = (f32[64,64,256]{2,1,0:T(8,128)}, f32[64,64,256]{2,1,0:T(8,128)}) custom-call(s32[2]{0:T(128)} %pad_add_fusion.info, bf16[64,256,128]{2,1,0:T(8,128)(2,1)} %bitcast.78, bf16[64,256,512]{2,1,0:T(8,128)(2,1)} %bitcast.76), custom_call_target="tpu_custom_call" | custom-call | flops 5000000000 | bytes 20000000 | tf_op jit(solution)/shard_map/partial_0/pallas_call | solution.py:253
  353.2 11.6 %partial_1.1 = (f32[64,64,256]{2,1,0:T(8,128)}, f32[64,64,256]{2,1,0:T(8,128)}) custom-call(s32[2]{0:T(128)} %pad_add_fusion.info, bf16[64,256,128]{2,1,0:T(8,128)(2,1)} %bitcast.79, bf16[64,256,512]{2,1,0:T(8,128)(2,1)} %bitcast.77), custom_call_target="tpu_custom_call" | custom-call | flops 5000000000 | bytes 20000000 | tf_op jit(solution)/shard_map/partial_1/pallas_call | solution.py:253
  364.8 0.4 collective-permute-start
  365.2 0.9 convert_element_type.212.wg_ref
  366.1 0.6 convert_element_type.208
  366.7 1.0 copy.66.wo_ref
  367.9 1.0 broadcast_in_dim.139.ln_ref
  368.9 0.8 broadcast_in_dim.142.bo_ref
  369.7 0.8 broadcast_in_dim.145.bg_ref
  370.5 9.2 %second_layer_0.1.rest_0_ = bf16[64,64,512]{2,1,0:T(8,128)(2,1)} custom-call(s32[2]{0:T(128)} %pad_add_fusion.info, f32[64,64,256]{2,1,0:T(8,128)} %get-tuple-element.47.own_ref, f32[64,64,256]{2,1,0:T(8,128)} %collective-permute-done.1.got_ref, bf16[256,64,512]{2,1,0:T(8,128)(2,1)} %first_layer.1.z_ref, f32[2,64,256]{2,1,0:T(8,128)} %broadcast_in_dim.138.ln_ref.lni_ref, ...), custom_call_target="tpu_custom_call" | custom-call | flops 5000000000 | bytes 20000000 | tf_op jit(solution)/shard_map/second_layer_0/pallas_call | solution.py:292
  379.8 9.3 %second_layer_1.1 = bf16[64,64,512]{2,1,0:T(8,128)(2,1)} custom-call(s32[2]{0:T(128)} %pad_add_fusion.info, f32[64,64,256]{2,1,0:T(8,128)} %get-tuple-element.45.own_ref, f32[64,64,256]{2,1,0:T(8,128)} %collective-permute-done.got_ref, bf16[256,64,512]{2,1,0:T(8,128)(2,1)} %first_layer.1.z_ref, ...), custom_call_target="tpu_custom_call", output_to_operand_aliasing={{}: (10, {})} | custom-call | flops 5000000000 | bytes 20000000 | tf_op jit(solution)/shard_map/second_layer_1/pallas_call | solution.py:292
  (74 shorter events, 3.5 us)
Async XLA Ops:
  6.5 7.3 %copy-start.4 = (bf16[2,64,256]{2,1,0:T(8,128)(2,1)S(1)}, bf16[2,64,256]{2,1,0:T(8,128)(2,1)}, u32[]{:S(2)}) copy-start(bf16[2,64,256]{2,1,0:T(8,128)(2,1)} %param.13) | copy-start | bytes 196612
  6.5 46.0 %all-gather.10.cloned.1.call-start = ((), (), s32[]{:S(2)}) async-start(), calls=%async_computation | async-start | bytes 1179648 | tf_op jit(solution)/shard_map/all_gather | solution.py:347
  7.3 71.0 %all-gather.18.cloned.1.call-start = ((), (), s32[]{:S(2)}) async-start(), calls=%async_computation.4 | async-start | bytes 9437184 | tf_op jit(solution)/shard_map/all_gather | solution.py:356
  11.7 113.9 %all-gather.16.cloned.1.call-start = ((), (), s32[]{:S(2)}) async-start(), calls=%async_computation.3 | async-start | bytes 9437184 | tf_op jit(solution)/shard_map/all_gather | solution.py:356
  12.5 160.2 %all-gather.14.cloned.1.call-start = ((), (), s32[]{:S(2)}) async-start(), calls=%async_computation.2 | async-start | bytes 9437184 | tf_op jit(solution)/shard_map/all_gather | solution.py:356
  13.1 206.7 %all-gather.12.cloned.1.call-start = ((), (), s32[]{:S(2)}) async-start(), calls=%async_computation.1 | async-start | bytes 9437184 | tf_op jit(solution)/shard_map/all_gather | solution.py:356
  16.1 9.5 %copy-start.8 = (bf16[2,256]{1,0:T(2,128)(2,1)S(1)}, bf16[2,256]{1,0:T(2,128)(2,1)}, u32[]{:S(2)}) copy-start(bf16[2,256]{1,0:T(2,128)(2,1)} %param.14) | copy-start | bytes 3076
  23.3 21.9 %copy-start = (f32[1,4,256,256]{3,2,1,0:T(8,128)S(1)}, f32[1,4,256,256]{3,2,1,0:T(8,128)}, u32[]{:S(2)}) copy-start(f32[1,4,256,256]{3,2,1,0:T(8,128)} %mul.307) | copy-start | bytes 3145732
  23.3 21.9 %copy-start.1 = (f32[1,4,256,256]{3,2,1,0:T(8,128)S(1)}, f32[1,4,256,256]{3,2,1,0:T(8,128)}, u32[]{:S(2)}) copy-start(f32[1,4,256,256]{3,2,1,0:T(8,128)} %mul.274) | copy-start | bytes 3145732
  45.2 6.8 %copy-start.11 = (bf16[2,2,64]{2,1,0:T(2,128)(2,1)S(1)}, bf16[2,2,64]{2,1,0:T(2,128)(2,1)}, u32[]{:S(2)}) copy-start(bf16[2,2,64]{2,1,0:T(2,128)(2,1)} %param.12) | copy-start | bytes 1540
  45.2 6.8 %copy-start.12 = (bf16[2,2,64]{2,1,0:T(2,128)(2,1)S(1)}, bf16[2,2,64]{2,1,0:T(2,128)(2,1)}, u32[]{:S(2)}) copy-start(bf16[2,2,64]{2,1,0:T(2,128)(2,1)} %param.17) | copy-start | bytes 1540
  219.9 23.9 %copy-start.5 = (f32[512]{0:T(512)S(1)}, f32[512]{0:T(512)}, u32[]{:S(2)}) copy-start(f32[512]{0:T(512)} %broadcast_in_dim.126) | copy-start | bytes 6148
  219.9 24.8 %copy-start.6 = (f32[512]{0:T(512)S(1)}, f32[512]{0:T(512)}, u32[]{:S(2)}) copy-start(f32[512]{0:T(512)} %broadcast_in_dim.129) | copy-start | bytes 6148
  353.1 12.1 %copy-start.3 = (bf16[4,64,4,64]{3,2,1,0:T(4,128)(2,1)S(1)}, bf16[4,64,4,64]{3,2,1,0:T(4,128)(2,1)}, u32[]{:S(2)}) copy-start(bf16[4,64,4,64]{3,2,1,0:T(4,128)(2,1)} %get-tuple-element.69) | copy-start | bytes 393220
  353.1 13.0 %copy-start.2 = (bf16[8,64,64,8]{1,0,3,2:T(8,128)(2,1)S(1)}, bf16[8,64,64,8]{1,0,3,2:T(8,128)(2,1)}, u32[]{:S(2)}) copy-start(bf16[8,64,64,8]{1,0,3,2:T(8,128)(2,1)} %get-tuple-element.67) | copy-start | bytes 1572868
  353.1 14.6 %copy-start.9 = (f32[64]{0:T(128)S(1)}, f32[64]{0:T(128)}, u32[]{:S(2)}) copy-start(f32[64]{0:T(128)} %get-tuple-element.77) | copy-start | bytes 772
  353.1 14.7 %copy-start.10 = (f32[64]{0:T(128)S(1)}, f32[64]{0:T(128)}, u32[]{:S(2)}) copy-start(f32[64]{0:T(128)} %get-tuple-element.75) | copy-start | bytes 772
  353.1 14.7 %copy-start.7 = (f32[2,64]{1,0:T(2,128)S(1)}, f32[2,64]{1,0:T(2,128)}, u32[]{:S(2)}) copy-start(f32[2,64]{1,0:T(2,128)} %get-tuple-element.71) | copy-start | bytes 1540
  353.1 14.7 %collective-permute-start.1 = (f32[64,64,256]{2,1,0:T(8,128)}, f32[64,64,256]{2,1,0:T(8,128)}, u32[]{:S(2)}, u32[]{:S(2)}) collective-permute-start(f32[64,64,256]{2,1,0:T(8,128)} %get-tuple-element.48), channel_id=1, source_target_pairs={{0,1},{1,0},{2,3},{3,2},{4,5},{5,4},{6,7},{7,6},{8,9},{9,8},{10,11... | collective-permute-start | bytes 12582920 | tf_op jit(solution)/shard_map/ppermute | solution.py:370
  364.8 14.9 %collective-permute-start = (f32[64,64,256]{2,1,0:T(8,128)}, f32[64,64,256]{2,1,0:T(8,128)}, u32[]{:S(2)}, u32[]{:S(2)}) collective-permute-start(f32[64,64,256]{2,1,0:T(8,128)} %get-tuple-element.46), channel_id=1, source_target_pairs={{0,1},{1,0},{2,3},{3,2},{4,5},{5,4},{6,7},{7,6},{8,9},{9,8},{10,11... | collective-permute-start | bytes 12582920 | tf_op jit(solution)/shard_map/ppermute | solution.py:370
Sparse Core Ops, SparseCore 0:
  9.0 22.2 all-gather.9
  32.9 45.3 all-gather.17
  79.9 45.6 all-gather.15
  127.1 45.6 all-gather.13
  174.2 45.6 all-gather.11
